TPU v7x, 32 devices: a whole 2x2x4 slice. The times are simulated.
32 devices in a mesh: section: 2 (over core), seq: 4 (over y, x), head: 4 (over z).
Axes of the slice: x: 2, y: 2, z: 4, core: 2. Of those that a mesh axis runs over, the one named last changes fastest.
Arguments:
- x_in: bfloat16 [2, 1024, 8192], P('section', 'seq', 'head'), may hold values from -6 to 6
- b_in: bfloat16 [2, 1024, 2048], P('section', 'seq', 'head'), may hold values from -6 to 6
- c_in: bfloat16 [2, 1024, 2048], P('section', 'seq', 'head'), may hold values from -6 to 6
- z_in: bfloat16 [2, 1024, 8192], P('section', 'seq', 'head'), may hold values from -6 to 6
- dt_raw: float32 [2, 128, 1024], P('section', 'head', 'seq'), may hold values from -5 to 5
- conv_x: float32 [2, 4, 8192], P('section', None, 'head'), may hold values from -3 to 3
- conv_b: float32 [2, 4, 2048], P('section', None, 'head'), may hold values from -3 to 3
- conv_c: float32 [2, 4, 2048], P('section', None, 'head'), may hold values from -3 to 3
- a_rate: float32 [2, 128], P('section', 'head'), may hold values from 0.0001 to 1
- dt_bias: float32 [2, 128], P('section', 'head'), may hold values from -3 to -0.5
- skip_d: float32 [2, 128], P('section', 'head'), may hold values from 0.5 to 2
- norm_gain: float32 [2, 8192], P('section', 'head'), may hold values from 0.25 to 1.75
- out_weight: bfloat16 [2, 8192, 8192], P('section', 'head', 'seq'), may hold values from -0.0625 to 0.0625
Outputs:
- mixed: bfloat16 [2, 1024, 8192], P('section', ('seq', 'head'))
All inputs are finite; a program needn't handle non-finite values.
Results may differ from a plain program's by a relative error of at most 0.007.
Values may be sent and summed in bfloat16 or wider, within the bound.
A program may use at most 128 MiB of HBM per device.

v0:
```python
import jax
import jax.numpy as jnp
from jax import lax
from jax.sharding import PartitionSpec as P

N = 256
epsilon = 1e-05


def passed_along(block, axis, distance):
    devices = range(lax.axis_size(axis))
    route = [(i - distance, i) for i in devices if i - distance in devices]
    return lax.ppermute(block, axis, route)


def entering(decay, block, axis):
    size, place = (lax.axis_size(axis), lax.axis_index(axis))
    decays = lax.all_gather(decay, axis)
    blocks = lax.all_gather(block.astype(jnp.bfloat16), axis)
    carried = jnp.zeros_like(block)
    for k in range(size - 1):
        after = decays[k][:, :, None, None] * carried + blocks[k].astype(jnp.float32)
        carried = jnp.where(k < place, after, carried)
    return carried


def passed_along_2(block, axis, distance):
    devices = range(lax.axis_size(axis))
    route = [((i - distance) % len(devices), i) for i in devices]
    return lax.ppermute(block, axis, route)


def conv_silu(padded, kernel, length):
    kernel_taps = kernel.shape[0]
    summed = jnp.zeros((length, padded.shape[1]), jnp.float32)
    for offset in range(kernel_taps):
        summed = summed + kernel[offset] * padded[offset : offset + length].astype(jnp.float32)
    return jax.nn.silu(summed).astype(jnp.bfloat16)


def per_device(
    x_in,
    b_in,
    c_in,
    z_in,
    dt_raw,
    conv_x,
    conv_b,
    conv_c,
    a_rate,
    dt_bias,
    skip_d,
    norm_gain,
    out_weight,
):
    x_local = x_in[0]
    b_local = b_in[0]
    c_local = c_in[0]
    length = x_local.shape[0]
    kernel_taps = conv_x.shape[1]
    x_cols = x_local.shape[1]
    b_cols = b_local.shape[1]
    edge_rows = jnp.concatenate(
        [
            x_local[length - kernel_taps + 1 :],
            b_local[length - kernel_taps + 1 :],
            c_local[length - kernel_taps + 1 :],
        ],
        axis=1,
    )
    before = passed_along(edge_rows, "seq", 1)
    x_conv = conv_silu(jnp.concatenate([before[:, :x_cols], x_local], axis=0), conv_x[0], length)
    b_conv = conv_silu(
        jnp.concatenate([before[:, x_cols : x_cols + b_cols], b_local], axis=0), conv_b[0], length
    )
    c_conv = conv_silu(
        jnp.concatenate([before[:, x_cols + b_cols :], c_local], axis=0), conv_c[0], length
    )
    head_count = dt_raw.shape[1]
    group_count = b_cols // N
    per_group = head_count // group_count
    head_dim = x_cols // head_count
    step_size = jax.nn.softplus(dt_raw[0] + dt_bias[0][:, None])
    log_decay = jnp.cumsum(-a_rate[0][:, None] * step_size, axis=1)
    x_groups = x_conv.reshape(length, group_count, per_group, head_dim)
    b_groups = b_conv.reshape(length, group_count, N)
    c_groups = c_conv.reshape(length, group_count, N)
    log_groups = log_decay.reshape(group_count, per_group, length)
    step_groups = step_size.reshape(group_count, per_group, length)
    scores = jnp.einsum("tgn,ugn->gtu", c_groups, b_groups, preferred_element_type=jnp.float32)
    causal = jnp.arange(length)[:, None] >= jnp.arange(length)[None, :]
    spread_log = log_groups[:, :, :, None] - log_groups[:, :, None, :]
    damping = jnp.where(causal, jnp.exp(jnp.minimum(spread_log, 0.0)), 0.0)
    weights = (damping * step_groups[:, :, None, :] * scores[:, None]).astype(jnp.bfloat16)
    inside = jnp.einsum("gjtu,ugjp->tgjp", weights, x_groups, preferred_element_type=jnp.float32)
    to_end = jnp.exp(log_groups[:, :, -1:] - log_groups) * step_groups
    x_weighted = (
        x_groups.astype(jnp.float32) * jnp.transpose(to_end, (2, 0, 1))[..., None]
    ).astype(jnp.bfloat16)
    block_sum = jnp.einsum(
        "ugjp,ugn->gjpn", x_weighted, b_groups, preferred_element_type=jnp.float32
    )
    block_decay = jnp.exp(log_groups[:, :, -1])
    carried = entering(block_decay, block_sum, "seq")
    carried_b = carried.astype(jnp.bfloat16)
    outside = jnp.einsum("tgn,gjpn->tgjp", c_groups, carried_b, preferred_element_type=jnp.float32)
    outside = outside * jnp.transpose(jnp.exp(log_groups), (2, 0, 1))[..., None]
    skip_term = skip_d[0].reshape(group_count, per_group)
    out_ssm = inside + outside + skip_term[None, :, :, None] * x_groups.astype(jnp.float32)
    gate_act = jax.nn.silu(z_in[0].astype(jnp.float32)).reshape(
        length, group_count, per_group * head_dim
    )
    gated = out_ssm.reshape(length, group_count, per_group * head_dim) * gate_act
    inverse_rms = lax.rsqrt(jnp.mean(gated * gated, axis=2, keepdims=True) + epsilon)
    hidden = ((gated * inverse_rms).reshape(length, x_cols) * norm_gain[0]).astype(jnp.bfloat16)
    local_weight = out_weight[0]
    terms = jnp.dot(
        lax.all_gather(hidden, "seq", axis=0, tiled=True),
        local_weight,
        preferred_element_type=jnp.float32,
    )
    shards = lax.axis_size("seq")
    terms = terms.astype(jnp.bfloat16).reshape(shards, length, local_weight.shape[1])
    summed = lax.psum_scatter(terms, "head", scatter_dimension=1, tiled=True)
    spread = lax.all_to_all(summed, "seq", split_axis=0, concat_axis=2, tiled=True)
    mixed = spread.reshape(spread.shape[1], spread.shape[2])
    passed = passed_along_2(mixed, "section", 1)
    return passed[None]


def solution(mesh):
    return jax.shard_map(
        per_device,
        mesh=mesh,
        in_specs=(
            P("section", "seq", "head"),
            P("section", "seq", "head"),
            P("section", "seq", "head"),
            P("section", "seq", "head"),
            P("section", "head", "seq"),
            P("section", None, "head"),
            P("section", None, "head"),
            P("section", None, "head"),
            P("section", "head"),
            P("section", "head"),
            P("section", "head"),
            P("section", "head"),
            P("section", "head", "seq"),
        ),
        out_specs=P("section", ("seq", "head"), None),
        check_vma=False,
    )
```

profile of v0, /device:TPU:0, one launch (start us, length us, event | category | flops | bytes accessed | tf_op | source)
XLA Modules:
  0.0 265.6 jit_solution(9218574246040160207)
XLA Ops:
  6.5 0.0 all-gather.7.cloned.1.call-start
  6.5 0.9 slice_bitcast_fusion
  7.4 0.7 slice_bitcast_fusion.1
  8.1 4.9 %collective-permute-start = (bf16[3,3072]{1,0:T(4,128)(2,1)S(1)}, bf16[3,3072]{1,0:T(4,128)(2,1)S(1)}, u32[]{:S(2)}, u32[]{:S(2)}) collective-permute-start(bf16[3,3072]{1,0:T(4,128)(2,1)S(1)} %pad_maximum_fusion.3), channel_id=1, source_target_pairs={{0,4},{4,8},{8,12},{1,5},{5,9},{9,13},{2,6},{6,10},{10,14},{3,7},{... | collective-permute-start | bytes 55304 | tf_op jit(solution)/shard_map/ppermute | solution.py:13
  13.0 0.7 negate_bitcast_fusion
  13.7 0.5 broadcast.73
  14.2 1.3 reduce.9
  15.5 0.1 add.116
  15.6 0.8 squeeze.26
  16.3 0.7 fusion.47
  17.1 0.6 reduce-window.6
  17.7 0.2 slice_reduce_fusion
  17.9 0.1 broadcast_add_fusion
  18.1 0.1 slice.191
  18.1 0.1 copy.76
  18.2 0.9 fusion.50
  19.2 1.4 multiply_bitcast_fusion
  20.6 0.9 fusion.53
  21.4 0.0 collective-permute-done
  21.4 1.9 multiply_convert_fusion.5
  23.4 0.1 reshape.176
  23.5 0.0 copy-done.2
  23.5 1.5 multiply_convert_fusion.2
  25.0 0.5 copy.57
  25.5 0.0 copy-start.7
  25.5 0.0 copy-start
  25.5 1.4 convolution_convert_fusion
  26.9 0.0 all-gather.7.cloned.1.call-update
  27.0 0.0 all-gather.5.cloned.1.call-start
  27.0 0.0 copy-done.7
  27.1 0.6 reduce.10
  27.7 0.1 mul.316
  27.8 0.0 copy-done
  27.8 1.6 copy.67
  29.4 8.1 %all-gather = f32[8,16,1]{1,2,0:T(1,128)S(1)} all-gather(f32[2,16,1]{1,2,0:T(1,128)S(1)} %bitcast.125), channel_id=2, replica_groups=mesh['section'=2,'seq'=4,'head'=4] {'seq'}, dimensions={0}, use_global_device_ids=true | all-gather | bytes 640 | tf_op jit(solution)/shard_map/all_gather | solution.py:18
  37.5 0.0 copy-done.6
  37.5 0.0 copy-done.3
  37.5 0.4 multiply_convert_fusion.6
  37.9 0.1 reshape.175
  38.0 0.3 fusion.40
  38.2 41.8 %all-gather.7.cloned.1.call-done = bf16[8,16,64,256]{3,2,1,0:T(8,128)(2,1)} async-done(((bf16[2,16,64,256]{3,2,1,0:T(8,128)(2,1)}), bf16[8,16,64,256]{3,2,1,0:T(8,128)(2,1)}) %all-gather.7.cloned.1.call-update) | async-done | bytes 4194320 | tf_op jit(solution)/shard_map/all_gather | solution.py:19
  80.0 3.0 %fusion.31 = f32[2,16,64,256]{3,2,1,0:T(8,128)S(1)} fusion(bf16[8,16,64,256]{3,2,1,0:T(8,128)(2,1)} %all-gather.7.cloned.1.call-done, f32[2,16]{1,0:T(2,128)S(1)} %bitcast.128, f32[2,16]{1,0:T(2,128)S(1)} %bitcast.127, f32[2,16]{1,0:T(2,128)S(1)} %bitcast.126, pred[]{:T(512)S(6)} %gt.11, pred[]{:T(512)S(6)} %gt.10, pred[]{:T(512)S(6)} %gt.9, ...), kind=kOutput, calls=%fused_computation.43 | convolution fusion | flops 274726912 | bytes 5505411 | tf_op jit(solution)/shard_map/tgn,gjpn->tgjp/dot_general | solution.py:106
  83.0 0.0 copy-done.1
  83.0 0.0 copy-done.4
  83.0 4.5 %multiply_reduce_fusion = (f32[256,2]{0,1:T(2,128)S(1)}, f32[256,2,16,64]{0,3,2,1:T(8,128)}) fusion(f32[256,2,16,64]{0,3,2,1:T(8,128)S(1)} %bitcast.99, bf16[256,2,16,64]{0,3,2,1:T(8,128)(2,1)S(1)} %bitcast.103, f32[2,16]{1,0:T(2,128)S(1)} %mul.316, f32[256,2,16]{0,2,1:T(8,128)S(1)} %copy-done.4, f32[2,16,64,256]{3,2,1,0:T(8,128)S(1)} %fusion.31, ...), kind=kOutput, calls=%fused_computation.33 | convolution fusion | flops 287309312 | bytes 8030336 | tf_op jit(solution)/shard_map/gjtu,ugjp->tgjp/dot_general | solution.py:95
  87.5 1.9 copy.66
  89.4 0.1 copy.68
  89.6 0.6 mul.324
  90.2 0.0 copy-start.5
  90.2 0.9 copy.79
  91.1 0.0 copy-done.5
  91.1 1.8 fusion.26
  92.9 0.0 all-gather.5.cloned.1.call-update
  92.9 0.0 reduce-scatter.2.cloned.1.call-start
  92.9 52.7 %all-gather.5.cloned.1.call-done = bf16[1024,2048]{1,0:T(8,128)(2,1)} async-done(((bf16[256,2048]{1,0:T(8,128)(2,1)}), bf16[1024,2048]{1,0:T(8,128)(2,1)}) %all-gather.5.cloned.1.call-update) | async-done | bytes 4194320 | tf_op jit(solution)/shard_map/all_gather | solution.py:118
  145.6 13.8 %fusion.9 = bf16[1024,2048]{1,0:T(8,128)(2,1)} fusion(bf16[1024,2048]{1,0:T(8,128)(2,1)} %all-gather.5.cloned.1.call-done, bf16[1,2048,2048]{2,1,0:T(8,128)(2,1)} %param.25), kind=kOutput, calls=%fused_computation.10 | convolution fusion | flops 8592031744 | bytes 16777216 | tf_op jit(solution)/shard_map/dot_general | solution.py:117
  159.4 0.0 reduce-scatter.2.cloned.1.call-update
  159.4 77.0 %reduce-scatter.2.cloned.1.call-done = bf16[4,64,2048]{2,1,0:T(8,128)(2,1)} async-done(((bf16[4,256,2048]{2,1,0:T(8,128)(2,1)}), bf16[4,64,2048]{2,1,0:T(8,128)(2,1)}) %reduce-scatter.2.cloned.1.call-update) | async-done | bytes 1048592 | tf_op jit(solution)/shard_map/reduce_scatter | solution.py:124
  236.4 17.6 %all_to_all.15 = bf16[4,64,2048]{2,1,0:T(8,128)(2,1)S(1)} all-to-all(bf16[4,64,2048]{2,1,0:T(8,128)(2,1)} %reduce-scatter.2.cloned.1.call-done), channel_id=1, replica_groups=mesh['section'=2,'seq'=4,'head'=4] {'seq'}, dimensions={0} | all-to-all | bytes 2097152 | tf_op jit(solution)/shard_map/all_to_all | solution.py:125
  254.0 0.8 copy.69
  254.8 0.6 copy.80
  255.4 0.1 collective-permute-start.1
  255.5 2.6 collective-permute-done.1
  258.1 1.0 copy.97
  (17 shorter events, 0.2 us)
Async XLA Ops:
  6.5 16.9 %copy-start.2 = (bf16[1,256,2048]{2,1,0:T(8,128)(2,1)S(1)}, bf16[1,256,2048]{2,1,0:T(8,128)(2,1)}, u32[]{:S(2)}) copy-start(bf16[1,256,2048]{2,1,0:T(8,128)(2,1)} %param.13) | copy-start | bytes 3145732
  6.5 73.5 %all-gather.7.cloned.1.call-start = ((), (), s32[]{:S(2)}) async-start(), calls=%async_computation.4 | async-start | bytes 5242880 | tf_op jit(solution)/shard_map/all_gather | solution.py:19
  8.1 13.3 %collective-permute-start = (bf16[3,3072]{1,0:T(4,128)(2,1)S(1)}, bf16[3,3072]{1,0:T(4,128)(2,1)S(1)}, u32[]{:S(2)}, u32[]{:S(2)}) collective-permute-start(bf16[3,3072]{1,0:T(4,128)(2,1)S(1)} %pad_maximum_fusion.3), channel_id=1, source_target_pairs={{0,4},{4,8},{8,12},{1,5},{5,9},{9,13},{2,6},{6,10},{10,14},{3,7},{... | collective-permute-start | bytes 55304 | tf_op jit(solution)/shard_map/ppermute | solution.py:13
  25.5 1.6 copy-start.7
  25.5 2.3 copy-start
  26.9 10.6 %copy-start.6 = (f32[1,4,512]{2,1,0:T(4,128)S(1)}, f32[1,4,512]{2,1,0:T(4,128)}, u32[]{:S(2)}) copy-start(f32[1,4,512]{2,1,0:T(4,128)} %param.20) | copy-start | bytes 24580
  26.9 10.6 %copy-start.3 = (bf16[1,256,512]{2,1,0:T(8,128)(2,1)S(1)}, bf16[1,256,512]{2,1,0:T(8,128)(2,1)}, u32[]{:S(2)}) copy-start(bf16[1,256,512]{2,1,0:T(8,128)(2,1)} %param.15) | copy-start | bytes 786436
  27.0 118.6 %all-gather.5.cloned.1.call-start = ((), (), s32[]{:S(2)}) async-start(), calls=%async_computation.2 | async-start | bytes 5242880 | tf_op jit(solution)/shard_map/all_gather | solution.py:118
  80.0 3.0 %copy-start.1 = (f32[1,256,2048]{1,2,0:T(8,128)S(1)}, f32[1,256,2048]{1,2,0:T(8,128)}, u32[]{:S(2)}) copy-start(f32[1,256,2048]{1,2,0:T(8,128)} %copy.67) | copy-start | bytes 6291460
  80.0 3.0 %copy-start.4 = (f32[256,2,16]{0,2,1:T(8,128)S(1)}, f32[256,2,16]{0,2,1:T(8,128)}, u32[]{:S(2)}) copy-start(f32[256,2,16]{0,2,1:T(8,128)} %get-tuple-element.7) | copy-start | bytes 98308
  90.2 0.9 copy-start.5
  92.9 143.5 %reduce-scatter.2.cloned.1.call-start = ((), (), s32[]{:S(2)}) async-start(), calls=%async_computation.3 | async-start | bytes 5242880 | tf_op jit(solution)/shard_map/reduce_scatter | solution.py:124
  255.4 2.7 %collective-permute-start.1 = (bf16[64,8192]{1,0:T(8,128)(2,1)S(1)}, bf16[64,8192]{1,0:T(8,128)(2,1)S(1)}, u32[]{:S(2)}, u32[]{:S(2)}) collective-permute-start(bf16[64,8192]{1,0:T(8,128)(2,1)S(1)} %bitcast.104), channel_id=1, source_target_pairs={{16,0},{0,16},{17,1},{1,17},{18,2},{2,18},{19,3},{3,19},{20,4},{4,... | collective-permute-start | bytes 3145736 | tf_op jit(solution)/shard_map/ppermute | solution.py:30
Sparse Core Ops, SparseCore 0:
  27.1 52.8 all-gather.6
  93.0 52.5 all-gather.4
  159.6 76.7 reduce-scatter.1
where the time goes:
time: 266 us
  waiting for transfers between devices  174 us (65%)
  blocking collectives  25.7 us (10%)
  matrix products  22.9 us (9%)
  local copies, waits for them, and re-layouts  13.5 us (5%)
  between operations  13.4 us (5%)
  other arithmetic  11 us (4%)
  starting transfers between devices  5.03 us (2%)
    reduce_scatter x1, waiting for transfers between devices, per_device(): summed = lax.psum_scatter(terms, 'head', scatter_dimension=1, tiled=True)  77 us
    all_gather x1, waiting for transfers between devices, per_device(): lax.all_gather(hidden, 'seq', axis=0, tiled=True)  52.7 us
    all_gather x1, waiting for transfers between devices, entering(): blocks = lax.all_gather(block.astype(jnp.bfloat16), axis)  41.8 us
    all_to_all x1, blocking collectives, per_device(): lax.all_to_all(summed, 'seq', split_axis=0, concat_axis=2, tiled=True)  17.6 us
    dot_general x1, matrix products, per_device(): jnp.dot(lax.all_gather(hidden, 'seq', axis=0, tiled=True), local_weight,...  13.8 us
    all_gather x1, blocking collectives, entering(): decays = lax.all_gather(decay, axis)  8.08 us
  transfers between devices with their start and end apart: 5, of which 4 were waited for; matrix products, arithmetic and copies ran while one was open for 4% of the time, Pallas kernels for 0%

commit v1 on v0

--- a/solution.py
+++ b/solution.py
@@ -5,6 +5,33 @@
 
 N = 256
 epsilon = 1e-05
+
+
+def prepare_spans(inner_x, along_dim):
+    inner_x = jnp.moveaxis(inner_x, 0, along_dim)
+    piece_out = inner_x.shape
+    return inner_x.reshape(
+        *piece_out[:along_dim],
+        piece_out[along_dim] * piece_out[along_dim + 1],
+        *piece_out[along_dim + 2 :]
+    )
+
+
+def supply_group_by_axis(my_tile, net_axis):
+    extent = lax.axis_size(net_axis)
+    block_next = my_tile[None]
+    for hop_no in range(extent.bit_length() - 1):
+        now = 1 << hop_no
+        later = range(extent)
+        p_next = map(lambda s: (s, s ^ now), later)
+        even = list(p_next)
+        then = lax.ppermute(block_next, net_axis, even)
+        block_last = jnp.stack([block_next, then], 0)
+        arr_next = lax.axis_index(net_axis) >> hop_no & 1
+        block_next = jnp.where(arr_next == 0, block_last, block_last[::-1]).reshape(
+            -1, *my_tile.shape
+        )
+    return block_next
 
 
 def passed_along(block, axis, distance):
@@ -114,11 +141,12 @@
     inverse_rms = lax.rsqrt(jnp.mean(gated * gated, axis=2, keepdims=True) + epsilon)
     hidden = ((gated * inverse_rms).reshape(length, x_cols) * norm_gain[0]).astype(jnp.bfloat16)
     local_weight = out_weight[0]
-    terms = jnp.dot(
-        lax.all_gather(hidden, "seq", axis=0, tiled=True),
-        local_weight,
-        preferred_element_type=jnp.float32,
-    )
+
+    def set_zones(vals, local_block, pos_dim):
+        step_out = supply_group_by_axis(vals, local_block)
+        return prepare_spans(step_out, pos_dim)
+
+    terms = jnp.dot(set_zones(hidden, "seq", 0), local_weight, preferred_element_type=jnp.float32)
     shards = lax.axis_size("seq")
     terms = terms.astype(jnp.bfloat16).reshape(shards, length, local_weight.shape[1])
     summed = lax.psum_scatter(terms, "head", scatter_dimension=1, tiled=True)

time: 266 us -> 295 us (1.11)
  other arithmetic: 11 us -> 22.4 us
  local copies, waits for them, and re-layouts: 13.5 us -> 23.3 us
  waiting for transfers between devices: 174 us -> 182 us
  matrix products: 22.9 us -> 19.7 us
    ppermute x0 -> x2, waiting for transfers between devices: none -> 60.6 us  [supply_group_by_axis(): then = lax.ppermute(block_next, net_axis, even)]
    all_gather x1 -> x0, waiting for transfers between devices: 52.7 us -> none  [per_device(): lax.all_gather(hidden, 'seq', axis=0, tiled=True)]
    mul x1 -> x3, local copies, waits for them, and re-layouts: 0.61 us -> 6.26 us  [per_device(): gated * inverse_rms]
    another operation x3 -> x6, other arithmetic: 0.71 us -> 6.31 us  [the longest x3 5.61 us: supply_group_by_axis(): block_last = jnp.stack([block_next, then], 0)]
    convert_element_type x1 -> x2, other arithmetic: 1.77 us -> 6.29 us  [per_device(): ((gated * inverse_rms).reshape(length, x_cols) * norm_gain[0]).astype(jnp...]
    reshape x1 -> x2, local copies, waits for them, and re-layouts: 1.92 us -> 5.97 us  [per_device(): out_ssm.reshape(length, group_count, per_group * head_dim) * gate_act]
    dot_general x1, matrix products: 13.8 us -> 10.4 us  [per_device(): jnp.dot(set_zones(hidden, 'seq', 0), local_weight, preferred_element_type...]
  transfers between devices with their start and end apart: 5 -> 6, of which waited for: 4 -> 5; matrix products, arithmetic and copies ran while one was open for 4% -> 7% of each run, Pallas kernels for 0% -> 0%
where the time goes in v1:
time: 295 us
  waiting for transfers between devices  182 us (62%)
  blocking collectives  25.7 us (9%)
  local copies, waits for them, and re-layouts  23.3 us (8%)
  other arithmetic  22.4 us (8%)
  matrix products  19.7 us (7%)
  between operations  13.7 us (5%)
  starting transfers between devices  7.92 us (3%)
    reduce_scatter x1, waiting for transfers between devices, per_device(): summed = lax.psum_scatter(terms, 'head', scatter_dimension=1, tiled=True)  77 us
    ppermute x2, waiting for transfers between devices, supply_group_by_axis(): then = lax.ppermute(block_next, net_axis, even)  60.6 us
    all_gather x1, waiting for transfers between devices, entering(): blocks = lax.all_gather(block.astype(jnp.bfloat16), axis)  41.8 us
    all_to_all x1, blocking collectives, per_device(): lax.all_to_all(summed, 'seq', split_axis=0, concat_axis=2, tiled=True)  17.6 us
    dot_general x1, matrix products, per_device(): jnp.dot(set_zones(hidden, 'seq', 0), local_weight, preferred_element_type...  10.4 us
    all_gather x1, blocking collectives, entering(): decays = lax.all_gather(decay, axis)  8.08 us
    convert_element_type x2, other arithmetic, per_device(): ((gated * inverse_rms).reshape(length, x_cols) * norm_gain[0]).astype(jnp...  6.29 us
    mul x3, local copies, waits for them, and re-layouts, per_device(): gated * inverse_rms  6.26 us
  transfers between devices with their start and end apart: 6, of which 5 were waited for; matrix products, arithmetic and copies ran while one was open for 7% of the time, Pallas kernels for 0%

profile of v1, /device:TPU:0, one launch (start us, length us, event | category | flops | bytes accessed | tf_op | source)
XLA Modules:
  0.0 294.7 jit_solution(15944919457631648068)
XLA Ops:
  6.5 0.9 slice_bitcast_fusion
  7.4 0.7 slice_bitcast_fusion.1
  8.1 4.9 %collective-permute-start = (bf16[3,3072]{1,0:T(4,128)(2,1)S(1)}, bf16[3,3072]{1,0:T(4,128)(2,1)S(1)}, u32[]{:S(2)}, u32[]{:S(2)}) collective-permute-start(bf16[3,3072]{1,0:T(4,128)(2,1)S(1)} %pad_maximum_fusion.5), channel_id=1, source_target_pairs={{0,4},{4,8},{8,12},{1,5},{5,9},{9,13},{2,6},{6,10},{10,14},{3,7},{... | collective-permute-start | bytes 55304 | tf_op jit(solution)/shard_map/ppermute | solution.py:40
  13.0 0.9 fusion.52
  14.0 0.8 squeeze.26
  14.8 0.7 negate_bitcast_fusion
  15.4 0.7 fusion.49
  16.2 0.6 reduce-window.6
  16.8 0.2 slice_reduce_fusion
  17.0 0.1 broadcast_add_fusion
  17.1 0.1 slice.191
  17.2 0.1 copy.81
  17.3 0.5 broadcast.112
  17.8 1.2 reduce.9
  19.1 0.1 add.126
  19.1 1.4 multiply_bitcast_fusion
  20.5 0.9 fusion.55
  21.4 0.0 collective-permute-done
  21.4 1.9 multiply_convert_fusion.6
  23.3 0.1 reshape.264
  23.4 1.5 multiply_convert_fusion.3
  24.9 0.5 copy.61
  25.4 0.0 copy-start.8
  25.4 0.0 copy-start
  25.4 1.4 convolution_convert_fusion
  26.9 0.0 all-gather.4.cloned.1.call-update
  26.9 0.0 reduce-scatter.2.cloned.1.call-start
  27.0 0.6 reduce.10
  27.6 0.1 mul.360
  27.7 1.6 copy.71
  29.3 8.1 %all-gather = f32[8,16,1]{1,2,0:T(1,128)S(1)} all-gather(f32[2,16,1]{1,2,0:T(1,128)S(1)} %bitcast.132), channel_id=2, replica_groups=mesh['section'=2,'seq'=4,'head'=4] {'seq'}, dimensions={0}, use_global_device_ids=true | all-gather | bytes 640 | tf_op jit(solution)/shard_map/all_gather | solution.py:45
  37.4 0.4 multiply_convert_fusion.7
  37.8 0.1 reshape.263
  37.9 0.3 fusion.42
  38.1 41.8 %all-gather.4.cloned.1.call-done = bf16[8,16,64,256]{3,2,1,0:T(8,128)(2,1)} async-done(((bf16[2,16,64,256]{3,2,1,0:T(8,128)(2,1)}), bf16[8,16,64,256]{3,2,1,0:T(8,128)(2,1)}) %all-gather.4.cloned.1.call-update) | async-done | bytes 4194320 | tf_op jit(solution)/shard_map/all_gather | solution.py:46
  80.0 3.0 %fusion.33 = f32[2,16,64,256]{3,2,1,0:T(8,128)S(1)} fusion(bf16[8,16,64,256]{3,2,1,0:T(8,128)(2,1)} %all-gather.4.cloned.1.call-done, f32[2,16]{1,0:T(2,128)S(1)} %bitcast.135, f32[2,16]{1,0:T(2,128)S(1)} %bitcast.134, f32[2,16]{1,0:T(2,128)S(1)} %bitcast.133, pred[]{:T(512)S(6)} %gt.11, pred[]{:T(512)S(6)} %gt.10, pred[]{:T(512)S(6)} %gt.9, ...), kind=kOutput, calls=%fused_computation.50 | convolution fusion | flops 274726912 | bytes 5505411 | tf_op jit(solution)/shard_map/tgn,gjpn->tgjp/dot_general | solution.py:133
  82.9 4.7 %multiply_reduce_fusion = (f32[256,2]{0,1:T(2,128)S(1)}, f32[256,2,16,64]{0,3,2,1:T(8,128)}) fusion(f32[256,2,16,64]{0,3,2,1:T(8,128)S(1)} %bitcast.106, bf16[256,2,16,64]{0,3,2,1:T(8,128)(2,1)S(1)} %bitcast.109, f32[2,16]{1,0:T(2,128)S(1)} %mul.360, f32[256,2,16]{0,2,1:T(8,128)S(1)} %copy-done.6, f32[2,16,64,256]{3,2,1,0:T(8,128)S(1)} %fusion.33, ...), kind=kOutput, calls=%fused_computation.38 | convolution fusion | flops 287309312 | bytes 8030336 | tf_op jit(solution)/shard_map/gjtu,ugjp->tgjp/dot_general | solution.py:122
  87.6 0.1 copy.72
  87.8 0.6 mul.368
  88.4 2.8 mul.376
  91.2 2.9 copy.73
  94.1 3.9 %multiply_convert_fusion.2 = bf16[1,256,2048]{2,1,0:T(8,128)(2,1)} fusion(f32[1,256,2048]{2,1,0:T(8,128)} %mul.376, f32[1,256,2048]{2,1,0:T(8,128)} %copy.73, bf16[1,256,2048]{2,1,0:T(8,128)(2,1)S(1)} %copy-done, f32[2048]{0:T(1024)S(1)} %bitcast.117), kind=kLoop, calls=%fused_computation.37 | loop fusion | flops 4718592 | bytes 6299648 | tf_op jit(solution)/shard_map/convert_element_type | solution.py:142
  98.1 1.5 collective-permute-start.1
  99.5 2.8 mul.369
  102.4 3.1 %copy.70 = f32[1,1,256,2048]{3,2,1,0:T(8,128)} copy(f32[1,1,256,2048]{2,3,1,0:T(8,128)} %bitcast.99) | data formatting | bytes 4194304 | tf_op jit(solution)/shard_map/reshape | solution.py:140
  105.4 2.3 fusion.26
  107.8 15.4 %collective-permute-done.1 = bf16[1,256,2048]{2,1,0:T(8,128)(2,1)} collective-permute-done((bf16[1,256,2048]{2,1,0:T(8,128)(2,1)}, bf16[1,256,2048]{2,1,0:T(8,128)(2,1)}, u32[]{:S(2)}, u32[]{:S(2)}) %collective-permute-start.1) | collective-permute-done | bytes 1048608 | tf_op jit(solution)/shard_map/ppermute | solution.py:28
  123.1 1.4 pad_maximum_fusion.1
  124.5 2.1 fusion.28
  126.6 1.5 collective-permute-start.2
  128.1 45.2 %collective-permute-done.2 = bf16[2,256,2048]{2,1,0:T(8,128)(2,1)} collective-permute-done((bf16[2,256,2048]{2,1,0:T(8,128)(2,1)}, bf16[2,256,2048]{2,1,0:T(8,128)(2,1)}, u32[]{:S(2)}, u32[]{:S(2)}) %collective-permute-start.2) | collective-permute-done | bytes 2097184 | tf_op jit(solution)/shard_map/ppermute | solution.py:28
  173.3 2.1 pad_maximum_fusion
  175.4 0.0 slice-start.1
  175.4 1.4 reverse_select_fusion
  176.8 1.0 slice-done.1
  177.8 10.4 %fusion.9 = bf16[1024,2048]{1,0:T(8,128)(2,1)} fusion(bf16[1024,2048]{1,0:T(8,128)(2,1)S(1)} %bitcast.101, bf16[1,2048,2048]{2,1,0:T(8,128)(2,1)S(1)} %bitcast.138), kind=kOutput, calls=%fused_computation.12 | convolution fusion | flops 8592031744 | bytes 16777216 | tf_op jit(solution)/shard_map/dot_general | solution.py:149
  188.2 0.0 reduce-scatter.2.cloned.1.call-update
  188.2 77.0 %reduce-scatter.2.cloned.1.call-done = bf16[4,64,2048]{2,1,0:T(8,128)(2,1)} async-done(((bf16[4,256,2048]{2,1,0:T(8,128)(2,1)}), bf16[4,64,2048]{2,1,0:T(8,128)(2,1)}) %reduce-scatter.2.cloned.1.call-update) | async-done | bytes 1048592 | tf_op jit(solution)/shard_map/reduce_scatter | solution.py:152
  265.2 17.6 %all_to_all.15 = bf16[4,64,2048]{2,1,0:T(8,128)(2,1)S(1)} all-to-all(bf16[4,64,2048]{2,1,0:T(8,128)(2,1)} %reduce-scatter.2.cloned.1.call-done), channel_id=1, replica_groups=mesh['section'=2,'seq'=4,'head'=4] {'seq'}, dimensions={0} | all-to-all | bytes 2097152 | tf_op jit(solution)/shard_map/all_to_all | solution.py:153
  282.8 0.8 copy.74
  283.6 0.6 copy.84
  284.2 0.1 collective-permute-start.3
  284.3 2.6 collective-permute-done.3
  286.9 1.0 copy.101
  (32 shorter events, 0.2 us)
Async XLA Ops:
  6.5 16.9 %copy-start.3 = (bf16[1,256,2048]{2,1,0:T(8,128)(2,1)S(1)}, bf16[1,256,2048]{2,1,0:T(8,128)(2,1)}, u32[]{:S(2)}) copy-start(bf16[1,256,2048]{2,1,0:T(8,128)(2,1)} %param.13) | copy-start | bytes 3145732
  6.5 73.4 %all-gather.4.cloned.1.call-start = ((), (), s32[]{:S(2)}) async-start(), calls=%async_computation.3 | async-start | bytes 5242880 | tf_op jit(solution)/shard_map/all_gather | solution.py:46
  8.1 13.2 %collective-permute-start = (bf16[3,3072]{1,0:T(4,128)(2,1)S(1)}, bf16[3,3072]{1,0:T(4,128)(2,1)S(1)}, u32[]{:S(2)}, u32[]{:S(2)}) collective-permute-start(bf16[3,3072]{1,0:T(4,128)(2,1)S(1)} %pad_maximum_fusion.5), channel_id=1, source_target_pairs={{0,4},{4,8},{8,12},{1,5},{5,9},{9,13},{2,6},{6,10},{10,14},{3,7},{... | collective-permute-start | bytes 55304 | tf_op jit(solution)/shard_map/ppermute | solution.py:40
  25.4 1.6 copy-start.8
  25.4 2.2 copy-start
  26.9 10.5 %copy-start.7 = (f32[1,4,512]{2,1,0:T(4,128)S(1)}, f32[1,4,512]{2,1,0:T(4,128)}, u32[]{:S(2)}) copy-start(f32[1,4,512]{2,1,0:T(4,128)} %param.20) | copy-start | bytes 24580
  26.9 10.6 %copy-start.4 = (bf16[1,256,512]{2,1,0:T(8,128)(2,1)S(1)}, bf16[1,256,512]{2,1,0:T(8,128)(2,1)}, u32[]{:S(2)}) copy-start(bf16[1,256,512]{2,1,0:T(8,128)(2,1)} %param.15) | copy-start | bytes 786436
  26.9 238.3 %reduce-scatter.2.cloned.1.call-start = ((), (), s32[]{:S(2)}) async-start(), calls=%async_computation.2 | async-start | bytes 5242880 | tf_op jit(solution)/shard_map/reduce_scatter | solution.py:152
  80.0 3.0 %copy-start.2 = (f32[1,256,2048]{1,2,0:T(8,128)S(1)}, f32[1,256,2048]{1,2,0:T(8,128)}, u32[]{:S(2)}) copy-start(f32[1,256,2048]{1,2,0:T(8,128)} %copy.71) | copy-start | bytes 6291460
  80.0 3.0 %copy-start.6 = (f32[256,2,16]{0,2,1:T(8,128)S(1)}, f32[256,2,16]{0,2,1:T(8,128)}, u32[]{:S(2)}) copy-start(f32[256,2,16]{0,2,1:T(8,128)} %get-tuple-element.9) | copy-start | bytes 98308
  91.2 2.9 copy-start.5
  98.1 25.1 %collective-permute-start.1 = (bf16[1,256,2048]{2,1,0:T(8,128)(2,1)}, bf16[1,256,2048]{2,1,0:T(8,128)(2,1)}, u32[]{:S(2)}, u32[]{:S(2)}) collective-permute-start(bf16[1,256,2048]{2,1,0:T(8,128)(2,1)} %multiply_convert_fusion.2), channel_id=1, source_target_pairs={{0,4},{4,0},{8,12},{12,8},{1,5},{5,1},{9,13},{13,9},{2,6},{6,2},{1... | collective-permute-start | bytes 3145736 | tf_op jit(solution)/shard_map/ppermute | solution.py:28
  102.4 3.1 %copy-start.1 = (f32[1,1,256,2048]{3,2,1,0:T(8,128)S(1)}, f32[1,1,256,2048]{3,2,1,0:T(8,128)}, u32[]{:S(2)}) copy-start(f32[1,1,256,2048]{3,2,1,0:T(8,128)} %mul.369) | copy-start | bytes 6291460
  126.6 46.7 %collective-permute-start.2 = (bf16[2,256,2048]{2,1,0:T(8,128)(2,1)}, bf16[2,256,2048]{2,1,0:T(8,128)(2,1)}, u32[]{:S(2)}, u32[]{:S(2)}) collective-permute-start(bf16[2,256,2048]{2,1,0:T(8,128)(2,1)} %get-tuple-element.8), channel_id=1, source_target_pairs={{0,8},{4,12},{8,0},{12,4},{1,9},{5,13},{9,1},{13,5},{2,10},{6,14},... | collective-permute-start | bytes 6291464 | tf_op jit(solution)/shard_map/ppermute | solution.py:28
  173.3 3.5 %slice-start = ((s8[8388608]{0:T(1024)(128)(4,1)}), s8[4194304]{0:T(1024)(128)(4,1)S(1)}, s32[]{:S(2)}) async-start(s8[8388608]{0:T(1024)(128)(4,1)} %bitcast.137), calls=%async_computation.4 | async-start | bytes 8388608
  175.4 2.4 slice-start.1
  284.2 2.7 collective-permute-start.3
Sparse Core Ops, SparseCore 0:
  27.0 52.8 all-gather.3
  188.3 76.7 reduce-scatter.1
